TPU v7x, 32 devices: a whole 2x2x4 slice. The times are simulated.
32 devices in a mesh: dp: 8 (over z, y), head: 4 (over x, core).
Axes of the slice: x: 2, y: 2, z: 4, core: 2. Of those that a mesh axis runs over, the one named last changes fastest.
Arguments:
- tokens: bfloat16 [8, 6312, 768], P('dp', 'head'), may hold values from -6 to 6
- frames: int32 [8], P('dp'), may hold values from 4 to 16
- text_mask: int32 [8, 40], P('dp'), may hold values 0 or 1
- latents: bfloat16 [8, 128, 768], P('dp'), may hold values from -6 to 6
- cross_q: bfloat16 [768, 768], P('head'), may hold values from -0.21875 to 0.21875
- cross_kv: bfloat16 [2, 768, 768], P(None, 'head'), may hold values from -0.21875 to 0.21875
- cross_out: bfloat16 [768, 768], P('head'), may hold values from -3.5 to 3.5
- cross_up: bfloat16 [768, 3072], P(None, 'head'), may hold values from -0.21875 to 0.21875
- cross_down: bfloat16 [3072, 768], P('head'), may hold values from -0.109375 to 0.109375
- self_qkv: bfloat16 [3, 768, 768], P(None, 'head'), may hold values from -0.21875 to 0.21875
- self_out: bfloat16 [768, 768], P('head'), may hold values from -0.875 to 0.875
- self_up: bfloat16 [768, 3072], P(None, 'head'), may hold values from -0.21875 to 0.21875
- self_down: bfloat16 [3072, 768], P('head'), may hold values from -0.109375 to 0.109375
- head_bias: float32 [2, 2, 768], P(None, None, 'head'), may hold values from -1.8 to 1.8
- up_bias: float32 [2, 3072], P(None, 'head'), may hold values from -1.8 to 1.8
- out_bias: float32 [2, 2, 768], replicated, may hold values from -1.8 to 1.8
- norm_gain: float32 [5, 768], replicated, may hold values from 0.5 to 1.5
- norm_bias: float32 [5, 768], replicated, may hold values from -1.8 to 1.8
- latents_cot: float32 [8, 128, 768], P('dp'), may hold values from -6 to 6
Outputs:
- latents_out: float32 [8, 128, 768], P('dp')
- grad_tokens: bfloat16 [8, 6312, 768], P('dp', 'head')
- grad_latents: float32 [8, 128, 768], P('dp')
- grad_cross_q: float32 [768, 768], P('head', 'dp')
- grad_cross_kv: float32 [2, 768, 768], P(None, 'head', 'dp')
- grad_cross_out: float32 [768, 768], P('head', 'dp')
- grad_cross_up: float32 [768, 3072], P('dp', 'head')
- grad_cross_down: float32 [3072, 768], P('head', 'dp')
- grad_self_qkv: float32 [3, 768, 768], P(None, 'head', 'dp')
- grad_self_out: float32 [768, 768], P('head', 'dp')
- grad_self_up: float32 [768, 3072], P('dp', 'head')
- grad_self_down: float32 [3072, 768], P('head', 'dp')
- grad_head_bias: float32 [2, 2, 768], P(None, None, 'head')
- grad_up_bias: float32 [2, 3072], P(None, 'head')
- grad_out_bias: float32 [2, 2, 768], P(None, None, 'head')
- grad_norm_gain: float32 [5, 768], P(None, 'head')
- grad_norm_bias: float32 [5, 768], P(None, 'head')
Inputs may be any that keep to these rules, and one draw needn't show every extreme that they name: The patches of frames at or after frames[c] are padding.
All inputs are finite; a program needn't handle non-finite values. No bound on the sum of `text_mask` on one device may be relied on, other than what follows from the above.
Results may differ from a plain program's by a relative error of at most 0.018.
Values may be sent and summed in bfloat16 or wider, within the bound.
A program may use at most 128 MiB of HBM per device.

v0:
```python
from functools import partial
import jax
import jax.numpy as jnp
from jax import lax
from jax.sharding import PartitionSpec as P

HD = 64
P_SIZE = 392
F_MAX = 16
EPSILON = 1e-05
NEGATIVE = -1e30


def normed(tensor, gain_row, shift_row):
    row_mean = jnp.mean(tensor, axis=-1, keepdims=True)
    centered = tensor - row_mean
    spread = jnp.mean(centered * centered, axis=-1, keepdims=True)
    return centered * lax.rsqrt(spread + EPSILON) * gain_row + shift_row


def share_of(tensor, head_index, head_width):
    return lax.dynamic_slice_in_dim(tensor, head_index * head_width, head_width, tensor.ndim - 1)


def split_heads(tensor, heads_here):
    return tensor.reshape(
        tensor.shape[0], tensor.shape[1], heads_here, tensor.shape[2] // heads_here
    )


def merge_heads(tensor):
    return tensor.reshape(tensor.shape[0], tensor.shape[1], tensor.shape[2] * tensor.shape[3])


def join_heads(partial_sum):
    return lax.psum(partial_sum.astype(jnp.bfloat16), "head").astype(jnp.float32)


def join_back(partial_sum):
    return lax.psum(partial_sum.astype(jnp.bfloat16), "head").astype(jnp.float32)


def scores_of(queries, key_rows, usable):
    scores = jnp.einsum("qhe,khe->hqk", queries, key_rows, preferred_element_type=jnp.float32)
    return jnp.where(usable[None, None, :], scores, NEGATIVE)


def attend_parts(parts):
    queries, key_rows, values, usable = parts
    scores = scores_of(queries, key_rows, usable)
    row_max = jnp.max(scores, axis=-1, keepdims=True)
    powers = jnp.exp(scores - row_max)
    totals = jnp.sum(powers, axis=-1, keepdims=True)
    chances = (powers / totals).astype(jnp.bfloat16)
    mixture = jnp.einsum("hqk,khe->qhe", chances, values, preferred_element_type=jnp.float32)
    return (mixture.astype(jnp.bfloat16), row_max, totals)


def back_parts(parts):
    queries, key_rows, values, usable, row_max, totals, grad_mix = parts
    scores = scores_of(queries, key_rows, usable)
    chances = jnp.exp(scores - row_max) / totals
    rounded = chances.astype(jnp.bfloat16)
    grad_values = jnp.einsum(
        "hqk,qhe->khe", rounded, grad_mix, preferred_element_type=jnp.float32
    ).astype(jnp.bfloat16)
    grad_chances = jnp.einsum("qhe,khe->hqk", grad_mix, values, preferred_element_type=jnp.float32)
    inner_sum = jnp.sum(chances * grad_chances, axis=-1, keepdims=True)
    grad_scores = (chances * (grad_chances - inner_sum)).astype(jnp.bfloat16)
    grad_queries = jnp.einsum(
        "hqk,khe->qhe", grad_scores, key_rows, preferred_element_type=jnp.float32
    ).astype(jnp.bfloat16)
    grad_keys = jnp.einsum(
        "hqk,qhe->khe", grad_scores, queries, preferred_element_type=jnp.float32
    ).astype(jnp.bfloat16)
    return (grad_queries, grad_keys, grad_values)


def feed_forward(tensor, gain_row, shift_row, weight_up, bias_up, weight_down):
    hidden = normed(tensor, gain_row, shift_row).astype(jnp.bfloat16)
    pre_act = (
        jnp.einsum("cnd,df->cnf", hidden, weight_up, preferred_element_type=jnp.float32) + bias_up
    )
    activation = jax.nn.gelu(pre_act, approximate=True).astype(jnp.bfloat16)
    partial_sum = jnp.einsum(
        "cnf,fd->cnd", activation, weight_down, preferred_element_type=jnp.float32
    )
    return (join_heads(partial_sum), (hidden, pre_act, activation))


def feed_back(tensor, gain_row, shift_row, weight_up, weight_down, saved_acts, grad_out):
    hidden, pre_act, activation = saved_acts
    grad_branch = grad_out.astype(jnp.bfloat16)
    grad_weight_down = jnp.einsum(
        "cnf,cnd->fd", activation, grad_branch, preferred_element_type=jnp.float32
    )
    grad_act = jnp.einsum(
        "cnd,fd->cnf", grad_branch, weight_down, preferred_element_type=jnp.float32
    )
    unused, gelu_pull = jax.vjp(partial(jax.nn.gelu, approximate=True), pre_act)
    grad_pre = gelu_pull(grad_act)[0].astype(jnp.bfloat16)
    grad_weight_up = jnp.einsum("cnd,cnf->df", hidden, grad_pre, preferred_element_type=jnp.float32)
    grad_bias_up = jnp.sum(grad_pre.astype(jnp.float32), axis=(0, 1))
    grad_hidden = join_back(
        jnp.einsum("cnf,df->cnd", grad_pre, weight_up, preferred_element_type=jnp.float32)
    )
    unused_too, norm_pull = jax.vjp(normed, tensor, gain_row, shift_row)
    grad_tensor, grad_gain, grad_shift = norm_pull(grad_hidden)
    return (grad_tensor, grad_weight_up, grad_bias_up, grad_weight_down, grad_gain, grad_shift)


def local(
    tokens,
    frames,
    text_mask,
    latents,
    cross_q,
    cross_kv,
    cross_out,
    cross_up,
    cross_down,
    self_qkv,
    self_out,
    self_up,
    self_down,
    head_bias,
    up_bias,
    out_bias,
    norm_gain,
    norm_bias,
    latents_cot,
):
    head_index = lax.axis_index("head")
    head_width = cross_q.shape[0]
    heads_here = head_width // HD
    scaling = HD ** (-0.5)
    clips_here = tokens.shape[0]
    rows_here = tokens.shape[1]
    length = rows_here * lax.axis_size("head")
    position = jnp.arange(length, dtype=jnp.int32)
    text_full = jnp.concatenate(
        [jnp.zeros((clips_here, F_MAX * P_SIZE), jnp.int32), text_mask], axis=1
    )
    usable = (position[None, :] < frames[:, None] * P_SIZE) | (text_full == 1)
    gathered, weights_whole = (
        lax.all_gather(tokens, "head", axis=1, tiled=True),
        lax.all_gather(cross_kv, "head", axis=1, tiled=True),
    )
    full_rows = gathered.astype(jnp.float32)
    row_mean = jnp.mean(full_rows, axis=-1, keepdims=True)
    centered = full_rows - row_mean
    inverse = lax.rsqrt(jnp.mean(centered * centered, axis=-1, keepdims=True) + EPSILON)
    inputs = (centered * inverse * norm_gain[0] + norm_bias[0]).astype(jnp.bfloat16)
    key_value = jnp.einsum("cld,kwd->clkw", inputs, cross_kv, preferred_element_type=jnp.float32)
    key_rows = key_value[:, :, 0].astype(jnp.bfloat16)
    cross_values = (key_value[:, :, 1] + head_bias[0, 1]).astype(jnp.bfloat16)
    start_state = latents.astype(jnp.float32)
    latent_norm = normed(start_state, norm_gain[1], norm_bias[1]).astype(jnp.bfloat16)
    cross_queries = (
        (
            jnp.einsum("cnd,wd->cnw", latent_norm, cross_q, preferred_element_type=jnp.float32)
            + head_bias[0, 0]
        )
        * scaling
    ).astype(jnp.bfloat16)
    cross_parts = (
        split_heads(cross_queries, heads_here),
        split_heads(key_rows, heads_here),
        split_heads(cross_values, heads_here),
        usable,
    )
    cross_mix, cross_max, cross_totals = lax.map(attend_parts, cross_parts)
    cross_flat = merge_heads(cross_mix)
    after_cross = (
        start_state
        + join_heads(
            jnp.einsum("cnw,wd->cnd", cross_flat, cross_out, preferred_element_type=jnp.float32)
        )
        + out_bias[0, 0]
    )
    cross_branch, cross_saved = feed_forward(
        after_cross, norm_gain[2], norm_bias[2], cross_up, up_bias[0], cross_down
    )
    after_mlp = after_cross + cross_branch + out_bias[0, 1]
    self_norm = normed(after_mlp, norm_gain[3], norm_bias[3]).astype(jnp.bfloat16)
    triple = jnp.einsum("cnd,kwd->cnkw", self_norm, self_qkv, preferred_element_type=jnp.float32)
    self_queries = ((triple[:, :, 0] + head_bias[1, 0]) * scaling).astype(jnp.bfloat16)
    self_keys = triple[:, :, 1].astype(jnp.bfloat16)
    self_values = (triple[:, :, 2] + head_bias[1, 1]).astype(jnp.bfloat16)
    everyone = jnp.ones((clips_here, self_keys.shape[1]), dtype=bool)
    self_parts = (
        split_heads(self_queries, heads_here),
        split_heads(self_keys, heads_here),
        split_heads(self_values, heads_here),
        everyone,
    )
    self_mix, self_max, self_totals = lax.map(attend_parts, self_parts)
    self_flat = merge_heads(self_mix)
    after_self = (
        after_mlp
        + join_heads(
            jnp.einsum("cnw,wd->cnd", self_flat, self_out, preferred_element_type=jnp.float32)
        )
        + out_bias[1, 0]
    )
    self_branch, self_saved = feed_forward(
        after_self, norm_gain[4], norm_bias[4], self_up, up_bias[1], self_down
    )
    latents_out = after_self + self_branch + out_bias[1, 1]
    bias_self_mlp = jnp.sum(latents_cot, axis=(0, 1))
    grad_ln_four, grad_self_up, upbias_self, grad_self_down, gain_four, shift_four = feed_back(
        after_self, norm_gain[4], norm_bias[4], self_up, self_down, self_saved, latents_cot
    )
    grad_state = latents_cot + grad_ln_four
    bias_self_attn = jnp.sum(grad_state, axis=(0, 1))
    grad_attn_in = grad_state.astype(jnp.bfloat16)
    grad_self_out = jnp.einsum(
        "cnw,cnd->wd", self_flat, grad_attn_in, preferred_element_type=jnp.float32
    )
    grad_mix = jnp.einsum(
        "cnd,wd->cnw", grad_attn_in, self_out, preferred_element_type=jnp.float32
    ).astype(jnp.bfloat16)
    self_grads = lax.map(
        back_parts, self_parts + (self_max, self_totals, split_heads(grad_mix, heads_here))
    )
    grad_query_scaled = (merge_heads(self_grads[0]).astype(jnp.float32) * scaling).astype(
        jnp.bfloat16
    )
    grad_triple = jnp.stack(
        [grad_query_scaled, merge_heads(self_grads[1]), merge_heads(self_grads[2])], axis=2
    )
    grad_self_qkv = jnp.einsum(
        "cnd,cnkw->kwd", self_norm, grad_triple, preferred_element_type=jnp.float32
    )
    bias_self_q = jnp.sum(grad_triple[:, :, 0].astype(jnp.float32), axis=(0, 1))
    bias_self_v = jnp.sum(grad_triple[:, :, 2].astype(jnp.float32), axis=(0, 1))
    grad_self_in = join_back(
        jnp.einsum("cnkw,kwd->cnd", grad_triple, self_qkv, preferred_element_type=jnp.float32)
    )
    unused, norm_pull = jax.vjp(normed, after_mlp, norm_gain[3], norm_bias[3])
    grad_ln_three, gain_three, shift_three = norm_pull(grad_self_in)
    grad_state = grad_state + grad_ln_three
    bias_cross_mlp = jnp.sum(grad_state, axis=(0, 1))
    grad_ln_two, grad_cross_up, upbias_cross, grad_cross_down, gain_two, shift_two = feed_back(
        after_cross, norm_gain[2], norm_bias[2], cross_up, cross_down, cross_saved, grad_state
    )
    grad_state = grad_state + grad_ln_two
    bias_cross_attn = jnp.sum(grad_state, axis=(0, 1))
    grad_attn_in = grad_state.astype(jnp.bfloat16)
    grad_cross_out = jnp.einsum(
        "cnw,cnd->wd", cross_flat, grad_attn_in, preferred_element_type=jnp.float32
    )
    grad_mix = jnp.einsum(
        "cnd,wd->cnw", grad_attn_in, cross_out, preferred_element_type=jnp.float32
    ).astype(jnp.bfloat16)
    cross_grads = lax.map(
        back_parts, cross_parts + (cross_max, cross_totals, split_heads(grad_mix, heads_here))
    )
    grad_query_cross = (merge_heads(cross_grads[0]).astype(jnp.float32) * scaling).astype(
        jnp.bfloat16
    )
    grad_cross_q = jnp.einsum(
        "cnd,cnw->wd", latent_norm, grad_query_cross, preferred_element_type=jnp.float32
    )
    bias_cross_q = jnp.sum(grad_query_cross.astype(jnp.float32), axis=(0, 1))
    grad_latent_in = join_back(
        jnp.einsum("cnw,wd->cnd", grad_query_cross, cross_q, preferred_element_type=jnp.float32)
    )
    unused_too, latent_pull = jax.vjp(normed, start_state, norm_gain[1], norm_bias[1])
    grad_ln_one, gain_one, shift_one = latent_pull(grad_latent_in)
    grad_latents = grad_state + grad_ln_one
    grad_pair = jnp.stack([merge_heads(cross_grads[1]), merge_heads(cross_grads[2])], axis=2)
    grad_cross_kv = jnp.einsum(
        "cld,clkw->kwd", inputs, grad_pair, preferred_element_type=jnp.float32
    )
    bias_cross_v = jnp.sum(grad_pair[:, :, 1].astype(jnp.float32), axis=(0, 1))
    arrived = lax.all_to_all(grad_pair, "head", split_axis=1, concat_axis=3, tiled=True)
    grad_share = jnp.einsum(
        "clkw,kwd->cld", arrived, weights_whole, preferred_element_type=jnp.float32
    )
    own_start = head_index * rows_here
    own_mean = lax.dynamic_slice_in_dim(row_mean, own_start, rows_here, 1)
    own_inverse = lax.dynamic_slice_in_dim(inverse, own_start, rows_here, 1)
    standard = (tokens.astype(jnp.float32) - own_mean) * own_inverse
    scaled = grad_share * norm_gain[0]
    mean_plain = jnp.mean(scaled, axis=-1, keepdims=True)
    mean_cross = jnp.mean(scaled * standard, axis=-1, keepdims=True)
    grad_tokens = (own_inverse * (scaled - mean_plain - standard * mean_cross)).astype(jnp.bfloat16)
    gain_zero, shift_zero = lax.psum(
        (jnp.sum(grad_share * standard, axis=(0, 1)), jnp.sum(grad_share, axis=(0, 1))), "head"
    )
    grad_head_bias = jnp.stack(
        [jnp.stack([bias_cross_q, bias_cross_v]), jnp.stack([bias_self_q, bias_self_v])]
    )
    grad_up_bias = jnp.stack([upbias_cross, upbias_self])
    out_full = jnp.stack(
        [jnp.stack([bias_cross_attn, bias_cross_mlp]), jnp.stack([bias_self_attn, bias_self_mlp])]
    )
    grad_out_bias = share_of(out_full, head_index, head_width)
    grad_norm_gain = share_of(
        jnp.stack([gain_zero, gain_one, gain_two, gain_three, gain_four]), head_index, head_width
    )
    grad_norm_bias = share_of(
        jnp.stack([shift_zero, shift_one, shift_two, shift_three, shift_four]),
        head_index,
        head_width,
    )
    small_sums = lax.psum(
        (grad_head_bias, grad_up_bias, grad_out_bias, grad_norm_gain, grad_norm_bias), "dp"
    )
    pieces = [
        grad_cross_q.T,
        grad_cross_kv[0].T,
        grad_cross_kv[1].T,
        grad_cross_out.T,
        grad_self_qkv[0].T,
        grad_self_qkv[1].T,
        grad_self_qkv[2].T,
        grad_self_out.T,
        grad_cross_up,
        grad_cross_down.T,
        grad_self_up,
        grad_self_down.T,
    ]
    packed = jnp.concatenate([piece.astype(jnp.bfloat16) for piece in pieces], axis=1)
    summed = lax.psum_scatter(packed, "dp", scatter_dimension=0, tiled=True).astype(jnp.float32)
    sums = []
    start = 0
    for piece in pieces:
        sums.append(summed[:, start : start + piece.shape[1]])
        start += piece.shape[1]
    return (
        latents_out,
        grad_tokens,
        grad_latents,
        sums[0].T,
        jnp.stack([sums[1].T, sums[2].T]),
        sums[3].T,
        sums[8],
        sums[9].T,
        jnp.stack([sums[4].T, sums[5].T, sums[6].T]),
        sums[7].T,
        sums[10],
        sums[11].T,
        small_sums[0],
        small_sums[1],
        small_sums[2],
        small_sums[3],
        small_sums[4],
    )


def solution(mesh):
    in_specs = (
        P("dp", "head", None),
        P("dp"),
        P("dp", None),
        P("dp", None, None),
        P("head", None),
        P(None, "head", None),
        P("head", None),
        P(None, "head"),
        P("head", None),
        P(None, "head", None),
        P("head", None),
        P(None, "head"),
        P("head", None),
        P(None, None, "head"),
        P(None, "head"),
        P(),
        P(),
        P(),
        P("dp", None, None),
    )
    out_specs = (
        P("dp", None, None),
        P("dp", "head", None),
        P("dp", None, None),
        P("head", "dp"),
        P(None, "head", "dp"),
        P("head", "dp"),
        P("dp", "head"),
        P("head", "dp"),
        P(None, "head", "dp"),
        P("head", "dp"),
        P("dp", "head"),
        P("head", "dp"),
        P(None, None, "head"),
        P(None, "head"),
        P(None, None, "head"),
        P(None, "head"),
        P(None, "head"),
    )
    return jax.shard_map(local, mesh=mesh, in_specs=in_specs, out_specs=out_specs, check_vma=False)
```

profile of v0, /device:TPU:0, one launch (start us, length us, event | category | flops | bytes accessed | tf_op | source)
XLA Modules:
  0.0 712.1 jit_solution(15768888642467319990)
XLA Ops:
  7.3 18.4 %copy.67 = bf16[1,1578,768]{2,0,1:T(2,128)(2,1)} copy(bf16[1,1578,768]{2,1,0:T(8,128)(2,1)} %param.19) | data formatting | bytes 4847616 | tf_op args[0]
  28.8 122.7 %all-gather.3.cloned.1.call-done = bf16[1,6312,768]{2,0,1:T(2,128)(2,1)} async-done(((bf16[1,1578,768]{2,0,1:T(2,128)(2,1)}), bf16[1,6312,768]{2,0,1:T(2,128)(2,1)}) %all-gather.3.cloned.1.call-update) | async-done | bytes 9695248 | tf_op jit(solution)/shard_map/all_gather | solution.py:146
  151.5 7.5 %convert_reduce_fusion = f32[6312]{0:T(1024)S(1)} fusion(bf16[1,6312,768]{2,0,1:T(2,128)(2,1)} %all-gather.3.cloned.1.call-done), kind=kLoop, calls=%fused_computation.3 | loop fusion | flops 9688920 | bytes 9720480 | tf_op jit(solution)/shard_map/reduce_sum | solution.py:150
  159.0 14.1 %fusion.4 = f32[6312]{0:T(1024)S(1)} fusion(f32[6312]{0:T(1024)S(1)} %broadcast_multiply_fusion, bf16[1,6312,768]{2,0,1:T(2,128)(2,1)} %all-gather.3.cloned.1.call-done), kind=kLoop, calls=%fused_computation.6 | loop fusion | flops 19384152 | bytes 9745728 | tf_op jit(solution)/shard_map/reduce_sum | solution.py:152
  173.2 5.6 fusion.10
  188.3 6.2 fusion.167
  201.4 31.3 %all-reduce.12.cloned.1.call-done = bf16[1,128,768]{2,1,0:T(8,128)(2,1)} async-done(((bf16[1,128,768]{2,1,0:T(8,128)(2,1)}), bf16[1,128,768]{2,1,0:T(8,128)(2,1)}) %all-reduce.12.cloned.1.call-update) | async-done | bytes 196624 | tf_op jit(solution)/shard_map/psum | solution.py:36
  239.6 30.8 %all-reduce.14.cloned.1.call-done = bf16[1,128,768]{2,1,0:T(8,128)(2,1)} async-done(((bf16[1,128,768]{2,1,0:T(8,128)(2,1)}), bf16[1,128,768]{2,1,0:T(8,128)(2,1)}) %all-reduce.14.cloned.1.call-update) | async-done | bytes 196624 | tf_op jit(solution)/shard_map/psum | solution.py:36
  280.2 32.1 %all-reduce.16.cloned.1.call-done = bf16[1,128,768]{2,1,0:T(8,128)(2,1)} async-done(((bf16[1,128,768]{2,1,0:T(8,128)(2,1)}), bf16[1,128,768]{2,1,0:T(8,128)(2,1)}) %all-reduce.16.cloned.1.call-update) | async-done | bytes 196624 | tf_op jit(solution)/shard_map/psum | solution.py:36
  320.7 32.1 %all-reduce.18.cloned.1.call-done = bf16[1,128,768]{2,1,0:T(8,128)(2,1)} async-done(((bf16[1,128,768]{2,1,0:T(8,128)(2,1)}), bf16[1,128,768]{2,1,0:T(8,128)(2,1)}) %all-reduce.18.cloned.1.call-update) | async-done | bytes 196624 | tf_op jit(solution)/shard_map/psum | solution.py:40
  369.1 32.1 %all-reduce.20.cloned.1.call-done = bf16[1,128,768]{2,1,0:T(8,128)(2,1)} async-done(((bf16[1,128,768]{2,1,0:T(8,128)(2,1)}), bf16[1,128,768]{2,1,0:T(8,128)(2,1)}) %all-reduce.20.cloned.1.call-update) | async-done | bytes 196624 | tf_op jit(solution)/shard_map/psum | solution.py:40
  412.3 29.7 %all-reduce.22.cloned.1.call-done = bf16[1,128,768]{2,1,0:T(8,128)(2,1)} async-done(((bf16[1,128,768]{2,1,0:T(8,128)(2,1)}), bf16[1,128,768]{2,1,0:T(8,128)(2,1)}) %all-reduce.22.cloned.1.call-update) | async-done | bytes 196624 | tf_op jit(solution)/shard_map/psum | solution.py:40
  449.2 11.8 %multiply_reduce_fusion = (f32[3,128]{1,0:T(4,128)S(1)}, f32[3,128,6312]{1,2,0:T(8,128)}) fusion(f32[3,128,6312]{1,2,0:T(8,128)} %get-tuple-element.268, f32[3,128]{1,0:T(4,128)S(1)} %copy-done.87, bf16[128,3,64]{0,2,1:T(8,128)(2,1)S(1)} %bitcast.305, f32[6312,3,64]{0,2,1:T(8,128)} %bitcast.281, f32[3,64]{1,0:T(4,128)S(1)} %copy-done.98), kind=kOutput, calls=%fused_computation.16 | convolution fusion | flops 319942272 | bytes 24291072 | tf_op jit(solution)/shard_map/while/body/eval_jaxpr/qhe,khe->hqk/dot_general | solution.py:67
  461.0 9.9 %multiply_convert_fusion = bf16[3,128,6312]{1,2,0:T(8,128)(2,1)} fusion(f32[3,128,6312]{1,2,0:T(8,128)} %get-tuple-element.274, f32[3,128]{1,0:T(4,128)S(1)} %get-tuple-element.273, f32[3,128,6312]{1,2,0:T(8,128)} %get-tuple-element.268, f32[3,128]{1,0:T(4,128)S(1)} %copy-done.87), kind=kLoop, calls=%fused_computation.15 | loop fusion | flops 9695232 | bytes 24241152 | tf_op jit(solution)/shard_map/while/body/eval_jaxpr/convert_element_type | solution.py:69
  478.5 6.3 convert_reduce_fusion.1
  487.9 7.9 %fusion.26 = bf16[2,192,768]{2,1,0:T(8,128)(2,1)S(1)} fusion(bf16[6312,768,1]{1,0,2:T(8,128)(2,1)} %copy-done.8, bf16[1,6312,1,192]{1,3,2,0:T(8,128)(2,1)S(1)} %bitcast.282, bf16[1,6312,1,192]{1,3,2,0:T(8,128)(2,1)S(1)} %bitcast.277), kind=kOutput, calls=%fused_computation.50 | convolution fusion | flops 3725687808 | bytes 15132672 | tf_op jit(solution)/shard_map/cld,clkw->kwd/dot_general | solution.py:273
  507.9 10.3 %copy.85 = bf16[768,4608]{1,0:T(8,128)(2,1)} copy(bf16[768,4608]{0,1:T(8,128)(2,1)} %fusion.25) | data formatting | bytes 14155776
  518.2 5.6 pad_maximum_fusion
  523.8 16.4 %copy.73 = bf16[1,6312,2,192]{3,2,0,1:T(2,128)(2,1)} copy(bf16[1,6312,2,192]{1,3,2,0:T(8,128)(2,1)} %pad_maximum_fusion) | data formatting | bytes 9695232 | tf_op jit(solution)/shard_map/stack | solution.py:272
  552.7 65.7 %all-to-all-done = bf16[1,6312,2,192]{3,2,0,1:T(2,128)(2,1)} async-done(((bf16[1,6312,2,192]{3,2,0,1:T(2,128)(2,1)}), bf16[1,6312,2,192]{3,2,0,1:T(2,128)(2,1)}, u32[]{:S(2)}, u32[]{:S(2)}) %all-to-all-start) | async-done | bytes 4847648 | tf_op jit(solution)/shard_map/all_to_all | solution.py:277
  618.4 17.0 %copy.74 = bf16[1,4,1578,2,192]{2,4,1,3,0:T(8,128)(2,1)} copy(bf16[1,4,1578,2,192]{4,3,2,1,0:T(2,128)(2,1)} %bitcast.46) | data formatting | bytes 9695232 | tf_op jit(solution)/shard_map/all_to_all | solution.py:277
  635.4 9.5 %fusion.13 = (f32[768]{0:T(1024)S(1)}, f32[1578]{0:T(1024)S(1)}, f32[1578,768,1]{1,0,2:T(8,128)S(1)}) fusion(bf16[1,1578,768]{2,1,0:T(8,128)(2,1)} %param.19, f32[1578]{0:T(1024)S(1)} %dynamic_slice.65, f32[1578]{0:T(1024)S(1)} %dynamic_slice.64, f32[768]{0:T(1024)S(1)} %copy-done.44, bf16[1578,2,768]{0,2,1:T(8,128)(2,1)} %bitcast.279, ...), kind=kOutput, calls=%fused_computation.26 | convolution fusion | flops 3732662016 | bytes 14503416 | tf_op jit(solution)/shard_map/clkw,kwd->cld/dot_general | solution.py:278
  647.8 6.2 all-reduce.2
  654.1 38.3 %all-reduce.1 = (f32[2,2,192]{2,1,0:T(2,128)}, f32[2,768]{1,0:T(2,128)}, f32[2,2,192]{2,1,0:T(2,128)}, f32[5,192]{1,0:T(8,128)}, f32[5,192]{1,0:T(8,128)}) all-reduce(f32[2,2,192]{2,1,0:T(2,128)S(1)} %pad_maximum_fusion.4, f32[2,768]{1,0:T(2,128)S(1)} %pad_maximum_fusion.3, ...), channel_id=1, replica_groups=mesh['dp'=8,'head'=4] {'dp'}, use_global_device_ids=true, to_apply=%region_39.40 | all-reduce | flops 4992 | bytes 39936 | tf_op jit(solution)/shard_map/psum | solution.py:308
  (382 shorter events, 127.9 us)
Async XLA Ops:
  7.2 230.0 %copy-start = (bf16[768,768]{1,0:T(8,128)(2,1)S(1)}, bf16[768,768]{1,0:T(8,128)(2,1)}, u32[]{:S(2)}) copy-start(bf16[768,768]{1,0:T(8,128)(2,1)} %param.27) | copy-start | bytes 3538948
  7.3 144.2 %all-gather.3.cloned.1.call-start = ((), (), s32[]{:S(2)}) async-start(), calls=%async_computation.2 | async-start | bytes 24238080 | tf_op jit(solution)/shard_map/all_gather | solution.py:146
  25.7 207.0 %all-reduce.12.cloned.1.call-start = ((), (), s32[]{:S(2)}) async-start(), calls=%async_computation.3 | async-start | bytes 393216 | tf_op jit(solution)/shard_map/psum | solution.py:36
  25.9 168.6 %copy-start.97 = (f32[3,64]{1,0:T(4,128)}, f32[3,64]{1,0:T(4,128)S(1)}, u32[]{:S(2)}) copy-start(f32[3,64]{1,0:T(4,128)S(1)} %add.328) | copy-start | bytes 2308
  27.9 131.0 %copy-start.89 = (f32[768]{0:T(1024)}, f32[768]{0:T(1024)S(1)}, u32[]{:S(2)}) copy-start(f32[768]{0:T(1024)S(1)} %get-tuple-element.220) | copy-start | bytes 9220
  27.9 207.1 %copy-start.48 = (f32[768]{0:T(1024)}, f32[768]{0:T(1024)S(1)}, u32[]{:S(2)}) copy-start(f32[768]{0:T(1024)S(1)} %get-tuple-element.219) | copy-start | bytes 9220
  28.0 130.9 %copy-start.45 = (f32[768]{0:T(1024)}, f32[768]{0:T(1024)S(1)}, u32[]{:S(2)}) copy-start(f32[768]{0:T(1024)S(1)} %get-tuple-element.215) | copy-start | bytes 9220
  28.0 145.1 %copy-start.43 = (f32[768]{0:T(1024)}, f32[768]{0:T(1024)S(1)}, u32[]{:S(2)}) copy-start(f32[768]{0:T(1024)S(1)} %get-tuple-element.216) | copy-start | bytes 9220
  28.1 130.8 %copy-start.77 = (f32[128]{0:T(128)}, f32[128]{0:T(128)S(1)}, u32[]{:S(2)}) copy-start(f32[128]{0:T(128)S(1)} %broadcast_multiply_fusion.6) | copy-start | bytes 1540
  28.4 130.6 %copy-start.101 = (f32[128]{0:T(128)}, f32[128]{0:T(128)S(1)}, u32[]{:S(2)}) copy-start(f32[128]{0:T(128)S(1)} %fusion.86) | copy-start | bytes 1540
  28.4 130.6 %copy-start.94 = (f32[128]{0:T(128)}, f32[128]{0:T(128)S(1)}, u32[]{:S(2)}) copy-start(f32[128]{0:T(128)S(1)} %fusion.133) | copy-start | bytes 1540
  28.7 154.8 %copy-start.35 = (bf16[128,192]{0,1:T(8,128)(2,1)}, bf16[128,192]{0,1:T(8,128)(2,1)S(1)}, u32[]{:S(2)}) copy-start(bf16[128,192]{0,1:T(8,128)(2,1)S(1)} %fusion.44) | copy-start | bytes 147460
  200.6 69.8 %all-reduce.14.cloned.1.call-start = ((), (), s32[]{:S(2)}) async-start(), calls=%async_computation.4 | async-start | bytes 393216 | tf_op jit(solution)/shard_map/psum | solution.py:36
  238.2 74.1 %all-reduce.16.cloned.1.call-start = ((), (), s32[]{:S(2)}) async-start(), calls=%async_computation.5 | async-start | bytes 393216 | tf_op jit(solution)/shard_map/psum | solution.py:36
  280.1 72.6 %all-reduce.18.cloned.1.call-start = ((), (), s32[]{:S(2)}) async-start(), calls=%async_computation.6 | async-start | bytes 393216 | tf_op jit(solution)/shard_map/psum | solution.py:40
  320.6 82.5 %copy-start.53 = (f32[128]{0:T(128)S(1)}, f32[128]{0:T(128)}, u32[]{:S(2)}) copy-start(f32[128]{0:T(128)} %copy-done.52) | copy-start | bytes 1540
  320.6 82.5 %copy-start.75 = (f32[128]{0:T(128)S(1)}, f32[128]{0:T(128)}, u32[]{:S(2)}) copy-start(f32[128]{0:T(128)} %copy-done.74) | copy-start | bytes 1540
  320.6 86.1 %copy-start.15 = (f32[128,768]{1,0:T(8,128)S(1)}, f32[128,768]{1,0:T(8,128)}, u32[]{:S(2)}) copy-start(f32[128,768]{1,0:T(8,128)} %copy-done.14) | copy-start | bytes 1179652
  320.6 80.6 %all-reduce.20.cloned.1.call-start = ((), (), s32[]{:S(2)}) async-start(), calls=%async_computation.7 | async-start | bytes 393216 | tf_op jit(solution)/shard_map/psum | solution.py:40
  369.1 72.9 %all-reduce.22.cloned.1.call-start = ((), (), s32[]{:S(2)}) async-start(), calls=%async_computation.8 | async-start | bytes 393216 | tf_op jit(solution)/shard_map/psum | solution.py:40
  409.8 138.4 %all-reduce.24.cloned.1.call-start = ((), (), s32[]{:S(2)}) async-start(), calls=%async_computation.11 | async-start | bytes 786432 | tf_op jit(solution)/shard_map/psum | solution.py:36
  476.8 158.6 %all-gather.5.cloned.1.call-start = ((), (), s32[]{:S(2)}) async-start(), calls=%async_computation.9 | async-start | bytes 2949120 | tf_op jit(solution)/shard_map/all_gather | solution.py:147
  477.5 220.0 %reduce-scatter.4.cloned.1.call-start = ((), (), s32[]{:S(2)}) async-start(), calls=%async_computation.10 | async-start | bytes 7962624
  540.4 78.0 %all-to-all-start = ((bf16[1,6312,2,192]{3,2,0,1:T(2,128)(2,1)}), bf16[1,6312,2,192]{3,2,0,1:T(2,128)(2,1)}, u32[]{:S(2)}, u32[]{:S(2)}) async-start(bf16[1,6312,2,192]{3,2,0,1:T(2,128)(2,1)} %copy.73), calls=%async_computation | async-start | bytes 12926976 | tf_op jit(solution)/shard_map/all_to_all | solution.py:277
  (97 other events, 1553.0 us)
Sparse Core Ops, SparseCore 0:
  25.9 125.5 all-gather.2
  200.7 32.0 all-reduce.11
  238.3 32.0 all-reduce.13
  280.3 32.0 all-reduce.15
  320.7 31.9 all-reduce.17
  369.2 32.0 all-reduce.19
  409.9 32.0 all-reduce.21
  476.9 32.9 all-reduce.23
  511.4 24.0 all-gather.4
  539.0 129.7 reduce-scatter.3
where the time goes:
time: 720 us; the launch traced here: 712 us
  waiting for transfers between devices  377 us (52%)
  matrix products  95.7 us (13%)
  local copies, waits for them, and re-layouts  86.2 us (12%)
  other arithmetic  85.1 us (12%)
  blocking collectives  44.6 us (6%)
  between operations  16.6 us (2%)
    all_gather x1, waiting for transfers between devices, local(): lax.all_gather(tokens, 'head', axis=1, tiled=True)  123 us
    psum x4, waiting for transfers between devices, join_heads(): lax.psum(partial_sum.astype(jnp.bfloat16), 'head').astype(jnp.float32)  94.3 us
    psum x3, waiting for transfers between devices, join_back(): lax.psum(partial_sum.astype(jnp.bfloat16), 'head').astype(jnp.float32)  93.9 us
    all_to_all x1, waiting for transfers between devices, local(): lax.all_to_all(grad_pair, 'head', split_axis=1, concat_axis=3, tiled=True)  65.7 us
    unnamed x232, local copies, waits for them, and re-layouts  45.2 us
    psum x1, blocking collectives, local(): lax.psum((grad_head_bias, grad_up_bias, grad_out_bias, grad_norm_gain, gr...  38.3 us
    all_to_all x1, local copies, waits for them, and re-layouts, local(): lax.all_to_all(grad_pair, 'head', split_axis=1, concat_axis=3, tiled=True)  17 us
    another operation x1, local copies, waits for them, and re-layouts, local(): jnp.stack([merge_heads(cross_grads[1]), merge_heads(cross_grads[2])], axi...  16.4 us
  transfers between devices with their start and end apart: 11, of which 8 were waited for; matrix products, arithmetic and copies ran while one was open for 15% of the time, Pallas kernels for 0%

commit v1 on v0

--- a/solution.py
+++ b/solution.py
@@ -9,6 +9,22 @@
 F_MAX = 16
 EPSILON = 1e-05
 NEGATIVE = -1e30
+
+
+def collect(x, axis, dim):
+    ways, here, step = (lax.axis_size(axis), lax.axis_index(axis), x.shape[dim])
+    shape = [n * ways if d == dim else n for d, n in enumerate(x.shape)]
+    full = lax.dynamic_update_slice_in_dim(jnp.zeros(shape, x.dtype), x, here * step, axis=dim)
+    going_up = going_down = x
+    for far in range(1, ways // 2 + 1):
+        going_up = lax.ppermute(going_up, axis, [(d, (d + 1) % ways) for d in range(ways)])
+        full = lax.dynamic_update_slice_in_dim(full, going_up, (here - far) % ways * step, axis=dim)
+        if 2 * far < ways:
+            going_down = lax.ppermute(going_down, axis, [(d, (d - 1) % ways) for d in range(ways)])
+            full = lax.dynamic_update_slice_in_dim(
+                full, going_down, (here + far) % ways * step, axis=dim
+            )
+    return full
 
 
 def normed(tensor, gain_row, shift_row):
@@ -143,7 +159,7 @@
     )
     usable = (position[None, :] < frames[:, None] * P_SIZE) | (text_full == 1)
     gathered, weights_whole = (
-        lax.all_gather(tokens, "head", axis=1, tiled=True),
+        collect(tokens, "head", 1),
         lax.all_gather(cross_kv, "head", axis=1, tiled=True),
     )
     full_rows = gathered.astype(jnp.float32)

time: 720 us -> 672 us (0.933)
  waiting for transfers between devices: 377 us -> 310 us
  local copies, waits for them, and re-layouts: 86.2 us -> 121 us
  other arithmetic: 85.1 us -> 68.3 us
    all_gather x1 -> x0, waiting for transfers between devices: 123 us -> none  [local(): lax.all_gather(tokens, 'head', axis=1, tiled=True)]
    ppermute x0 -> x3, waiting for transfers between devices: none -> 51 us  [the longest x2 51 us: collect(): lax.ppermute(going_up, axis, [(d, (d + 1) % ways) for d in range(ways)])]
    dynamic_update_slice x0 -> x4, local copies, waits for them, and re-layouts: none -> 49.9 us  [the longest x2 24.7 us: collect(): lax.dynamic_update_slice_in_dim(full, going_up, (here - far) % ways * ste...]
    unnamed x232 -> x261, local copies, waits for them, and re-layouts: 45.2 us -> 26.8 us
    reduce_sum x1, other arithmetic: 14.1 us -> 5.23 us  [local(): jnp.mean(centered * centered, axis=-1, keepdims=True) + EPSILON]
  transfers between devices with their start and end apart: 11 -> 13, of which waited for: 8 -> 8; matrix products, arithmetic and copies ran while one was open for 15% -> 22% of each run, Pallas kernels for 0% -> 0%
where the time goes in v1:
time: 672 us; the launch traced here: 665 us
  waiting for transfers between devices  310 us (46%)
  local copies, waits for them, and re-layouts  121 us (18%)
  matrix products  93.6 us (14%)
  other arithmetic  68.3 us (10%)
  blocking collectives  44.3 us (7%)
  between operations  16.5 us (2%)
  starting transfers between devices  11.2 us (2%)
    psum x4, waiting for transfers between devices, join_heads(): lax.psum(partial_sum.astype(jnp.bfloat16), 'head').astype(jnp.float32)  97.5 us
    psum x3, waiting for transfers between devices, join_back(): lax.psum(partial_sum.astype(jnp.bfloat16), 'head').astype(jnp.float32)  93.9 us
    all_to_all x1, waiting for transfers between devices, local(): lax.all_to_all(grad_pair, 'head', split_axis=1, concat_axis=3, tiled=True)  67 us
    ppermute x2, waiting for transfers between devices, collect(): lax.ppermute(going_up, axis, [(d, (d + 1) % ways) for d in range(ways)])  51 us
    psum x1, blocking collectives, local(): lax.psum((grad_head_bias, grad_up_bias, grad_out_bias, grad_norm_gain, gr...  38.2 us
    unnamed x261, local copies, waits for them, and re-layouts  26.8 us
    dynamic_update_slice x2, local copies, waits for them, and re-layouts, collect(): lax.dynamic_update_slice_in_dim(full, going_up, (here - far) % ways * ste...  24.7 us
    all_to_all x1, local copies, waits for them, and re-layouts, local(): lax.all_to_all(grad_pair, 'head', split_axis=1, concat_axis=3, tiled=True)  17 us
  transfers between devices with their start and end apart: 13, of which 8 were waited for; matrix products, arithmetic and copies ran while one was open for 22% of the time, Pallas kernels for 0%

profile of v1, /device:TPU:0, one launch (start us, length us, event | category | flops | bytes accessed | tf_op | source)
XLA Modules:
  0.0 664.8 jit_solution(2277514992694341858)
XLA Ops:
  9.8 51.0 %collective-permute-done = bf16[1,1578,768]{2,1,0:T(8,128)(2,1)} collective-permute-done((bf16[1,1578,768]{2,1,0:T(8,128)(2,1)}, bf16[1,1578,768]{2,1,0:T(8,128)(2,1)}, u32[]{:S(2)}, u32[]{:S(2)}) %collective-permute-start) | collective-permute-done | bytes 2423840 | tf_op jit(solution)/shard_map/ppermute | solution.py:20
  69.2 12.7 %dynamic_update_slice.39 = bf16[1,6312,768]{2,1,0:T(8,128)(2,1)} dynamic-update-slice(bf16[1,6312,768]{2,1,0:T(8,128)(2,1)} %broadcast_in_dim.155, bf16[1,1578,768]{2,1,0:T(8,128)(2,1)} %param.19, s32[]{:T(128)} %constant.158.clone.1, s32[]{:T(128)S(6)} %select_n.46, s32[]{:T(128)} %constant.158.clone.1) | dynamic-update-slice | bytes 4847620 | tf_op jit(solution)/shard_map/dynamic_update_slice | solution.py:17
  83.5 12.1 %dynamic_update_slice.40 = bf16[1,6312,768]{2,1,0:T(8,128)(2,1)} dynamic-update-slice(bf16[1,6312,768]{2,1,0:T(8,128)(2,1)} %dynamic_update_slice.39, bf16[1,1578,768]{2,1,0:T(8,128)(2,1)} %collective-permute-done, s32[]{:T(128)} %constant.158.clone.1, s32[]{:T(128)S(6)} %select_n.48, s32[]{:T(128)} %constant.158.clone.1) | dynamic-update-slice | bytes 4847620 | tf_op jit(solution)/shard_map/dynamic_update_slice | solution.py:21
  95.6 12.6 %dynamic_update_slice.41 = bf16[1,6312,768]{2,1,0:T(8,128)(2,1)} dynamic-update-slice(bf16[1,6312,768]{2,1,0:T(8,128)(2,1)} %dynamic_update_slice.40, bf16[1,1578,768]{2,1,0:T(8,128)(2,1)} %collective-permute-done.1, s32[]{:T(128)} %constant.158.clone.1, s32[]{:T(128)S(6)} %select_n.50, s32[]{:T(128)} %constant.158.clone.1) | dynamic-update-slice | bytes 4847620 | tf_op jit(solution)/shard_map/dynamic_update_slice | solution.py:24
  108.2 12.6 %dynamic_update_slice.42 = bf16[1,6312,768]{2,1,0:T(8,128)(2,1)} dynamic-update-slice(bf16[1,6312,768]{2,1,0:T(8,128)(2,1)} %dynamic_update_slice.41, bf16[1,1578,768]{2,1,0:T(8,128)(2,1)} %collective-permute-done.2, s32[]{:T(128)} %constant.158.clone.1, s32[]{:T(128)S(6)} %select_n.52, s32[]{:T(128)} %constant.158.clone.1) | dynamic-update-slice | bytes 4847620 | tf_op jit(solution)/shard_map/dynamic_update_slice | solution.py:21
  143.1 6.3 fusion.169
  149.4 6.4 fusion.45
  157.4 33.4 %all-reduce.12.cloned.1.call-done = bf16[1,128,768]{2,1,0:T(8,128)(2,1)} async-done(((bf16[1,128,768]{2,1,0:T(8,128)(2,1)}), bf16[1,128,768]{2,1,0:T(8,128)(2,1)}) %all-reduce.12.cloned.1.call-update) | async-done | bytes 196624 | tf_op jit(solution)/shard_map/psum | solution.py:52
  196.9 32.0 %all-reduce.14.cloned.1.call-done = bf16[1,128,768]{2,1,0:T(8,128)(2,1)} async-done(((bf16[1,128,768]{2,1,0:T(8,128)(2,1)}), bf16[1,128,768]{2,1,0:T(8,128)(2,1)}) %all-reduce.14.cloned.1.call-update) | async-done | bytes 196624 | tf_op jit(solution)/shard_map/psum | solution.py:52
  233.3 32.1 %all-reduce.16.cloned.1.call-done = bf16[1,128,768]{2,1,0:T(8,128)(2,1)} async-done(((bf16[1,128,768]{2,1,0:T(8,128)(2,1)}), bf16[1,128,768]{2,1,0:T(8,128)(2,1)}) %all-reduce.16.cloned.1.call-update) | async-done | bytes 196624 | tf_op jit(solution)/shard_map/psum | solution.py:52
  275.0 32.1 %all-reduce.18.cloned.1.call-done = bf16[1,128,768]{2,1,0:T(8,128)(2,1)} async-done(((bf16[1,128,768]{2,1,0:T(8,128)(2,1)}), bf16[1,128,768]{2,1,0:T(8,128)(2,1)}) %all-reduce.18.cloned.1.call-update) | async-done | bytes 196624 | tf_op jit(solution)/shard_map/psum | solution.py:56
  322.5 32.1 %all-reduce.20.cloned.1.call-done = bf16[1,128,768]{2,1,0:T(8,128)(2,1)} async-done(((bf16[1,128,768]{2,1,0:T(8,128)(2,1)}), bf16[1,128,768]{2,1,0:T(8,128)(2,1)}) %all-reduce.20.cloned.1.call-update) | async-done | bytes 196624 | tf_op jit(solution)/shard_map/psum | solution.py:56
  367.4 29.7 %all-reduce.22.cloned.1.call-done = bf16[1,128,768]{2,1,0:T(8,128)(2,1)} async-done(((bf16[1,128,768]{2,1,0:T(8,128)(2,1)}), bf16[1,128,768]{2,1,0:T(8,128)(2,1)}) %all-reduce.22.cloned.1.call-update) | async-done | bytes 196624 | tf_op jit(solution)/shard_map/psum | solution.py:56
  403.3 11.8 %multiply_reduce_fusion = (f32[3,128]{1,0:T(4,128)S(1)}, f32[3,128,6312]{1,2,0:T(8,128)}) fusion(f32[3,128,6312]{1,2,0:T(8,128)} %get-tuple-element.251, f32[3,128]{1,0:T(4,128)S(1)} %copy-done.99, bf16[128,3,64]{0,2,1:T(8,128)(2,1)S(1)} %bitcast.307, f32[6312,3,64]{0,2,1:T(8,128)} %bitcast.283, f32[3,64]{1,0:T(4,128)S(1)} %copy-done.111), kind=kOutput, calls=%fused_computation.16 | convolution fusion | flops 319942272 | bytes 24291072 | tf_op jit(solution)/shard_map/while/body/eval_jaxpr/qhe,khe->hqk/dot_general | solution.py:83
  415.1 9.9 %multiply_convert_fusion = bf16[3,128,6312]{1,2,0:T(8,128)(2,1)} fusion(f32[3,128,6312]{1,2,0:T(8,128)} %get-tuple-element.257, f32[3,128]{1,0:T(4,128)S(1)} %get-tuple-element.256, f32[3,128,6312]{1,2,0:T(8,128)} %get-tuple-element.251, f32[3,128]{1,0:T(4,128)S(1)} %copy-done.99), kind=kLoop, calls=%fused_computation.15 | loop fusion | flops 9695232 | bytes 24241152 | tf_op jit(solution)/shard_map/while/body/eval_jaxpr/convert_element_type | solution.py:85
  432.6 5.7 convert_reduce_fusion.1
  440.9 6.6 fusion.26
  460.9 10.5 %copy.71 = bf16[768,4608]{1,0:T(8,128)(2,1)} copy(bf16[768,4608]{0,1:T(8,128)(2,1)} %fusion.25) | data formatting | bytes 14155776
  477.0 16.4 %copy.59 = bf16[1,6312,2,192]{3,2,0,1:T(2,128)(2,1)} copy(bf16[1,6312,2,192]{1,3,2,0:T(8,128)(2,1)} %pad_maximum_fusion) | data formatting | bytes 9695232 | tf_op jit(solution)/shard_map/stack | solution.py:288
  504.4 67.0 %all-to-all-done = bf16[1,6312,2,192]{3,2,0,1:T(2,128)(2,1)} async-done(((bf16[1,6312,2,192]{3,2,0,1:T(2,128)(2,1)}), bf16[1,6312,2,192]{3,2,0,1:T(2,128)(2,1)}, u32[]{:S(2)}, u32[]{:S(2)}) %all-to-all-start) | async-done | bytes 4847648 | tf_op jit(solution)/shard_map/all_to_all | solution.py:293
  571.4 17.0 %copy.60 = bf16[1,4,1578,2,192]{2,4,1,3,0:T(8,128)(2,1)} copy(bf16[1,4,1578,2,192]{4,3,2,1,0:T(2,128)(2,1)} %bitcast.46) | data formatting | bytes 9695232 | tf_op jit(solution)/shard_map/all_to_all | solution.py:293
  588.4 9.7 %fusion.13 = (f32[768]{0:T(1024)S(1)}, f32[1578]{0:T(1024)S(1)}, f32[1578,768,1]{1,0,2:T(8,128)S(1)}) fusion(bf16[1,1578,768]{2,1,0:T(8,128)(2,1)} %param.19, f32[1578]{0:T(1024)S(1)} %dynamic_slice.65, f32[1578]{0:T(1024)S(1)} %dynamic_slice.64, f32[768]{0:T(1024)S(1)} %copy-done.57, bf16[1578,2,768]{0,2,1:T(8,128)(2,1)} %bitcast.281, ...), kind=kOutput, calls=%fused_computation.26 | convolution fusion | flops 3732662016 | bytes 14503416 | tf_op jit(solution)/shard_map/clkw,kwd->cld/dot_general | solution.py:294
  601.0 6.1 all-reduce.2
  607.3 38.2 %all-reduce.1 = (f32[2,2,192]{2,1,0:T(2,128)}, f32[2,768]{1,0:T(2,128)}, f32[2,2,192]{2,1,0:T(2,128)}, f32[5,192]{1,0:T(8,128)}, f32[5,192]{1,0:T(8,128)}) all-reduce(f32[2,2,192]{2,1,0:T(2,128)S(1)} %pad_maximum_fusion.4, f32[2,768]{1,0:T(2,128)S(1)} %pad_maximum_fusion.3, ...), channel_id=1, replica_groups=mesh['dp'=8,'head'=4] {'dp'}, use_global_device_ids=true, to_apply=%region_39.40 | all-reduce | flops 4992 | bytes 39936 | tf_op jit(solution)/shard_map/psum | solution.py:324
  (419 shorter events, 144.2 us)
Async XLA Ops:
  7.2 188.4 %copy-start = (bf16[768,768]{1,0:T(8,128)(2,1)S(1)}, bf16[768,768]{1,0:T(8,128)(2,1)}, u32[]{:S(2)}) copy-start(bf16[768,768]{1,0:T(8,128)(2,1)} %param.27) | copy-start | bytes 3538948
  7.2 183.5 %all-reduce.12.cloned.1.call-start = ((), (), s32[]{:S(2)}) async-start(), calls=%async_computation.2 | async-start | bytes 393216 | tf_op jit(solution)/shard_map/psum | solution.py:52
  7.3 53.6 %collective-permute-start = (bf16[1,1578,768]{2,1,0:T(8,128)(2,1)}, bf16[1,1578,768]{2,1,0:T(8,128)(2,1)}, u32[]{:S(2)}, u32[]{:S(2)}) collective-permute-start(bf16[1,1578,768]{2,1,0:T(8,128)(2,1)} %param.19), channel_id=1, source_target_pairs={{0,1},{1,2},{2,3},{3,0},{4,5},{5,6},{6,7},{7,4},{8,9},{9,10},{10,1... | collective-permute-start | bytes 7271432 | tf_op jit(solution)/shard_map/ppermute | solution.py:20
  7.8 87.8 %collective-permute-start.1 = (bf16[1,1578,768]{2,1,0:T(8,128)(2,1)}, bf16[1,1578,768]{2,1,0:T(8,128)(2,1)}, u32[]{:S(2)}, u32[]{:S(2)}) collective-permute-start(bf16[1,1578,768]{2,1,0:T(8,128)(2,1)} %param.19), channel_id=1, source_target_pairs={{0,3},{1,0},{2,1},{3,2},{4,7},{5,4},{6,5},{7,6},{8,11},{9,8},{10,9... | collective-permute-start | bytes 7271432 | tf_op jit(solution)/shard_map/ppermute | solution.py:23
  60.8 47.4 %collective-permute-start.2 = (bf16[1,1578,768]{2,1,0:T(8,128)(2,1)}, bf16[1,1578,768]{2,1,0:T(8,128)(2,1)}, u32[]{:S(2)}, u32[]{:S(2)}) collective-permute-start(bf16[1,1578,768]{2,1,0:T(8,128)(2,1)} %collective-permute-done), channel_id=1, source_target_pairs={{0,1},{1,2},{2,3},{3,0},{4,5},{5,6},{6,7},{7,4},{8,9},{9,10},{10,1... | collective-permute-start | bytes 7271432 | tf_op jit(solution)/shard_map/ppermute | solution.py:20
  64.1 85.3 %copy-start.110 = (f32[3,64]{1,0:T(4,128)}, f32[3,64]{1,0:T(4,128)S(1)}, u32[]{:S(2)}) copy-start(f32[3,64]{1,0:T(4,128)S(1)} %add.361) | copy-start | bytes 2308
  82.6 110.4 %copy-start.60 = (f32[768]{0:T(1024)}, f32[768]{0:T(1024)S(1)}, u32[]{:S(2)}) copy-start(f32[768]{0:T(1024)S(1)} %get-tuple-element.202) | copy-start | bytes 9220
  82.7 147.6 %copy-start.62 = (f32[768]{0:T(1024)}, f32[768]{0:T(1024)S(1)}, u32[]{:S(2)}) copy-start(f32[768]{0:T(1024)S(1)} %get-tuple-element.205) | copy-start | bytes 9220
  82.7 184.6 %copy-start.58 = (f32[768]{0:T(1024)}, f32[768]{0:T(1024)S(1)}, u32[]{:S(2)}) copy-start(f32[768]{0:T(1024)S(1)} %get-tuple-element.201) | copy-start | bytes 9220
  82.8 276.1 %copy-start.49 = (f32[768]{0:T(1024)}, f32[768]{0:T(1024)S(1)}, u32[]{:S(2)}) copy-start(f32[768]{0:T(1024)S(1)} %get-tuple-element.200) | copy-start | bytes 9220
  82.8 318.6 %copy-start.47 = (f32[768]{0:T(1024)}, f32[768]{0:T(1024)S(1)}, u32[]{:S(2)}) copy-start(f32[768]{0:T(1024)S(1)} %get-tuple-element.197) | copy-start | bytes 9220
  156.8 72.0 %all-reduce.14.cloned.1.call-start = ((), (), s32[]{:S(2)}) async-start(), calls=%async_computation.3 | async-start | bytes 393216 | tf_op jit(solution)/shard_map/psum | solution.py:52
  191.9 209.4 %copy-start.66 = (f32[128]{0:T(128)}, f32[128]{0:T(128)S(1)}, u32[]{:S(2)}) copy-start(f32[128]{0:T(128)S(1)} %broadcast_multiply_fusion.5) | copy-start | bytes 1540
  196.7 68.7 %all-reduce.16.cloned.1.call-start = ((), (), s32[]{:S(2)}) async-start(), calls=%async_computation.4 | async-start | bytes 393216 | tf_op jit(solution)/shard_map/psum | solution.py:52
  230.0 128.9 %copy-start.64 = (f32[128]{0:T(128)}, f32[128]{0:T(128)S(1)}, u32[]{:S(2)}) copy-start(f32[128]{0:T(128)S(1)} %broadcast_multiply_fusion.4) | copy-start | bytes 1540
  230.8 82.6 %copy-start.33 = (bf16[1,128,1,192]{1,3,2,0:T(8,128)(2,1)}, bf16[1,128,1,192]{1,3,2,0:T(8,128)(2,1)S(1)}, u32[]{:S(2)}) copy-start(bf16[1,128,1,192]{1,3,2,0:T(8,128)(2,1)S(1)} %slice.249) | copy-start | bytes 147460
  233.2 73.9 %all-reduce.18.cloned.1.call-start = ((), (), s32[]{:S(2)}) async-start(), calls=%async_computation.5 | async-start | bytes 393216 | tf_op jit(solution)/shard_map/psum | solution.py:56
  272.5 84.6 %copy-start.85 = (f32[128]{0:T(128)S(1)}, f32[128]{0:T(128)}, u32[]{:S(2)}) copy-start(f32[128]{0:T(128)} %copy-done.84) | copy-start | bytes 1540
  275.0 79.6 %all-reduce.20.cloned.1.call-start = ((), (), s32[]{:S(2)}) async-start(), calls=%async_computation.6 | async-start | bytes 393216 | tf_op jit(solution)/shard_map/psum | solution.py:56
  322.4 74.6 %all-reduce.22.cloned.1.call-start = ((), (), s32[]{:S(2)}) async-start(), calls=%async_computation.7 | async-start | bytes 393216 | tf_op jit(solution)/shard_map/psum | solution.py:56
  364.9 134.9 %all-reduce.24.cloned.1.call-start = ((), (), s32[]{:S(2)}) async-start(), calls=%async_computation.10 | async-start | bytes 786432 | tf_op jit(solution)/shard_map/psum | solution.py:52
  431.0 157.4 %all-gather.2.cloned.1.call-start = ((), (), s32[]{:S(2)}) async-start(), calls=%async_computation.8 | async-start | bytes 2949120 | tf_op jit(solution)/shard_map/all_gather | solution.py:163
  431.8 218.7 %reduce-scatter.4.cloned.1.call-start = ((), (), s32[]{:S(2)}) async-start(), calls=%async_computation.9 | async-start | bytes 7962624
  493.6 77.9 %all-to-all-start = ((bf16[1,6312,2,192]{3,2,0,1:T(2,128)(2,1)}), bf16[1,6312,2,192]{3,2,0,1:T(2,128)(2,1)}, u32[]{:S(2)}, u32[]{:S(2)}) async-start(bf16[1,6312,2,192]{3,2,0,1:T(2,128)(2,1)} %copy.59), calls=%async_computation | async-start | bytes 12926976 | tf_op jit(solution)/shard_map/all_to_all | solution.py:293
  (114 other events, 2053.2 us)
Sparse Core Ops, SparseCore 0:
  157.0 33.7 all-reduce.11
  196.8 32.0 all-reduce.13
  233.3 32.0 all-reduce.15
  275.1 31.9 all-reduce.17
  322.5 32.0 all-reduce.19
  365.0 31.9 all-reduce.21
  431.1 32.9 all-reduce.23
  465.6 24.0 all-gather.1
  493.4 129.8 reduce-scatter.3
